TPU v7x, 512 devices: a whole 4x8x8 slice. The times are simulated.
512 devices in a mesh: dp: 8 (over x, core), expert: 64 (over y, z).
Axes of the slice: x: 4, y: 8, z: 8, core: 2. Of those that a mesh axis runs over, the one named last changes fastest.
Arguments:
- cotangent: bfloat16 [65536, 3584], P(('dp', 'expert')), may hold values from -0.59765625 to 0.59765625
- expert_ids: int32 [65536, 1], P(('dp', 'expert')), may hold values from 0 to 15; in each aligned block of 128 rows (0 to 127, 128 to 255, ...) at most 12 rows name the same one
- route_weights: float32 [65536, 1], P(('dp', 'expert')), may hold values from 0.1 to 1
- gate_pre: bfloat16 [6144, 16384], P('dp', 'expert'), may hold values from -5 to 5
- up_pre: bfloat16 [6144, 16384], P('dp', 'expert'), may hold values from -5 to 5
- down_weight: bfloat16 [3584, 16384], P('dp', 'expert'), may hold values from -0.1875 to 0.1875
Outputs:
- weight_grad: bfloat16 [3584, 16384], P('dp', 'expert')
- gate_grad: bfloat16 [6144, 16384], P('dp', 'expert')
- up_grad: bfloat16 [6144, 16384], P('dp', 'expert')
Inputs may be any that keep to these rules, and one draw needn't show every extreme that they name: `expert_ids`: each token names one expert. Among the tokens of one device, at most 12 name the same expert, and in every draw some expert is named by exactly 12 tokens of some device.
All inputs are finite; a program needn't handle non-finite values.
Results may differ from a plain program's by a relative error of at most 0.013.
Values may be sent and summed in bfloat16 or wider, within the bound.
A program may use at most 64 MiB of HBM per device.

v0:
```python
import jax
import jax.numpy as jnp
from jax import lax
from jax.sharding import PartitionSpec as P

SPLIT = 4


def sent_to_all(array, axis):
    copies = jnp.broadcast_to(array, (lax.axis_size(axis), *array.shape))
    return lax.all_to_all(copies, axis, split_axis=0, concat_axis=0, tiled=True)


def laid_out(parts, dim):
    parts = jnp.moveaxis(parts, 0, dim)
    lengths = parts.shape
    return parts.reshape(*lengths[:dim], lengths[dim] * lengths[dim + 1], *lengths[dim + 2 :])


def gathered_copies(array, axis, dim):
    parts = sent_to_all(array, axis)
    return laid_out(parts, dim)


def split_up(array, dim, count):
    before, after = (array.shape[:dim], array.shape[dim + 1 :])
    return jnp.moveaxis(array.reshape(*before, count, -1, *after), dim, 0)


def sum_at_owner(array, axis, dim):
    parts = split_up(array, dim, lax.axis_size(axis))
    arrived = lax.all_to_all(parts, axis, split_axis=0, concat_axis=0, tiled=True)
    return arrived.astype(jnp.float32).sum(axis=0)


def slot_buffer(cotangent, expert_ids, route_weights, experts, capacity):
    columns = lax.broadcasted_iota(jnp.int32, (1, 1, experts), 2)
    onehot = (expert_ids[:, :, None] == columns).astype(jnp.int32)
    touched = jnp.sum(onehot, axis=1)
    earlier = jnp.cumsum(touched, axis=0) - touched
    position = jnp.sum(onehot * earlier[:, None, :], axis=2)
    target = expert_ids * capacity + position
    places = lax.broadcasted_iota(jnp.int32, (1, 1, experts * capacity), 2)
    chosen = (target[:, :, None] == places).astype(jnp.float32)
    picker = jnp.sum(chosen, axis=1)
    slot_scale = jnp.sum(chosen * route_weights[:, :, None], axis=(0, 1))
    picked = lax.dot_general(
        picker.astype(jnp.bfloat16),
        cotangent,
        (((0,), (0,)), ((), ())),
        preferred_element_type=jnp.float32,
    )
    return (picked * slot_scale[:, None]).astype(jnp.bfloat16)


def activations(gate_rows, up_rows, upstream):
    gate_full = gate_rows.astype(jnp.float32)
    up_full = up_rows.astype(jnp.float32)
    sigmoid = jax.nn.sigmoid(gate_full)
    active = gate_full * sigmoid
    product = (active * up_full).astype(jnp.bfloat16)
    gate_grad = (upstream * up_full * sigmoid * (1.0 + gate_full * (1.0 - sigmoid))).astype(
        jnp.bfloat16
    )
    up_grad = (upstream * active).astype(jnp.bfloat16)
    return (product, gate_grad, up_grad)


def per_device(cotangent, expert_ids, route_weights, gate_pre, up_pre, down_weight):
    devices = lax.axis_size("expert")
    experts = devices // SPLIT
    capacity = gate_pre.shape[0] // devices
    width = cotangent.shape[1]
    buffer = slot_buffer(cotangent, expert_ids, route_weights, experts, capacity)
    copies = jnp.broadcast_to(
        buffer.reshape(experts, 1, capacity, width), (experts, SPLIT, capacity, width)
    )
    arrived = lax.all_to_all(
        copies.reshape(devices, capacity, width), "expert", split_axis=0, concat_axis=0, tiled=True
    )
    routed = arrived.reshape(devices * capacity, width)
    columns = routed
    upstream = jnp.dot(
        columns, gathered_copies(down_weight, "dp", 0), preferred_element_type=jnp.float32
    )
    product, gate_grad, up_grad = activations(gate_pre, up_pre, upstream)
    columns = routed
    weight_grad = sum_at_owner(
        lax.dot_general(
            columns, product, (((0,), (0,)), ((), ())), preferred_element_type=jnp.float32
        ).astype(jnp.bfloat16),
        "dp",
        0,
    ).astype(jnp.bfloat16)
    return (weight_grad, gate_grad, up_grad)


def solution(mesh):
    placed = (
        P(("dp", "expert"), None),
        P(("dp", "expert"), None),
        P(("dp", "expert"), None),
        P("dp", "expert"),
        P("dp", "expert"),
        P("dp", "expert"),
    )
    return jax.shard_map(
        per_device,
        mesh=mesh,
        in_specs=placed,
        out_specs=(P("dp", "expert"), P("dp", "expert"), P("dp", "expert")),
        check_vma=False,
    )
```

profile of v0, /device:TPU:40, one launch (start us, length us, event | category | flops | bytes accessed | tf_op | source)
XLA Modules:
  0.0 289.3 jit_solution(12877706505439761167)
XLA Ops:
  0.6 0.0 copy-start
  0.6 3.4 %fusion.16 = s32[128]{0:T(128)S(1)} fusion(s32[128]{0:T(128)} %bitcast.19), kind=kOutput, calls=%fused_computation.30 | output fusion | flops 274304 | bytes 1024 | tf_op jit(solution)/shard_map/jit(cumsum)/reduce_window_sum | solution.py:40
  4.0 0.7 fusion.14
  4.7 0.8 select_reduce_fusion
  5.5 0.0 copy-done
  5.5 1.7 fusion
  7.2 2.3 broadcast_in_dim.6
  9.4 1.0 broadcast_in_dim.7
  10.4 0.0 copy-start.2
  10.4 219.5 %all_to_all.15 = bf16[64,12,3584]{2,1,0:T(8,128)(2,1)} all-to-all(bf16[64,12,3584]{2,1,0:T(8,128)(2,1)S(1)} %bitcast.15), channel_id=1, replica_groups=mesh['dp'=8,'expert'=64] {'expert'}, dimensions={0} | all-to-all | bytes 11010048 | tf_op jit(solution)/shard_map/all_to_all | solution.py:78
  229.9 0.0 copy-done.2
  229.9 1.4 broadcast_in_dim.8
  231.3 3.6 %all-to-all-start.2 = ((bf16[8,448,256]{2,1,0:T(8,128)(2,1)}), bf16[8,448,256]{2,1,0:T(8,128)(2,1)S(1)}, u32[]{:S(2)}, u32[]{:S(2)}) async-start(bf16[8,448,256]{2,1,0:T(8,128)(2,1)} %broadcast_in_dim.8), calls=%async_computation.2 | async-start | bytes 3670016 | tf_op jit(solution)/shard_map/all_to_all | solution.py:11
  234.9 0.0 copy-start.3
  234.9 0.0 copy-start.4
  234.9 9.4 %reshape.194 = bf16[768,3584]{1,0:T(8,128)(2,1)} reshape(bf16[64,12,3584]{2,1,0:T(8,128)(2,1)} %all_to_all.15) | data formatting | bytes 11010048 | tf_op jit(solution)/shard_map/reshape | solution.py:81
  244.4 0.0 copy-done.3
  244.4 0.0 copy-done.4
  244.4 5.6 %convolution_convert_fusion = bf16[3584,256]{1,0:T(8,128)(2,1)} fusion(bf16[768,3584]{1,0:T(8,128)(2,1)} %reshape.194, bf16[768,256]{1,0:T(8,128)(2,1)S(1)} %copy-done.3, bf16[768,256]{1,0:T(8,128)(2,1)S(1)} %copy-done.4), kind=kOutput, calls=%fused_computation.1 | convolution fusion | flops 1411776512 | bytes 8126464 | tf_op jit(solution)/shard_map/dot_general | solution.py:89
  249.9 9.2 %all-to-all-done.2 = bf16[8,448,256]{2,1,0:T(8,128)(2,1)S(1)} async-done(((bf16[8,448,256]{2,1,0:T(8,128)(2,1)}), bf16[8,448,256]{2,1,0:T(8,128)(2,1)S(1)}, u32[]{:S(2)}, u32[]{:S(2)}) %all-to-all-start.2) | async-done | bytes 1835040 | tf_op jit(solution)/shard_map/all_to_all | solution.py:11
  259.2 0.0 copy-start.1
  259.2 1.2 copy-done.1
  260.4 3.6 %all-to-all-start.1 = ((bf16[8,448,256]{2,1,0:T(8,128)(2,1)}), bf16[8,448,256]{2,1,0:T(8,128)(2,1)S(1)}, u32[]{:S(2)}, u32[]{:S(2)}) async-start(bf16[8,448,256]{2,1,0:T(8,128)(2,1)} %bitcast.17), calls=%async_computation.1 | async-start | bytes 3670016 | tf_op jit(solution)/shard_map/all_to_all | solution.py:32
  264.0 5.7 %multiply_convert_fusion = (bf16[768,256]{1,0:T(8,128)(2,1)}, bf16[768,256]{1,0:T(8,128)(2,1)}) fusion(bf16[768,256]{1,0:T(8,128)(2,1)S(1)} %copy-done.4, bf16[768,256]{1,0:T(8,128)(2,1)S(1)} %copy-done.3, bf16[768,3584]{1,0:T(8,128)(2,1)} %reshape.194, bf16[3584,256]{1,0:T(8,128)(2,1)} %bitcast.16), kind=kOutput, calls=%fused_computation.16 | convolution fusion | flops 1412235264 | bytes 8912896 | tf_op jit(solution)/shard_map/dot_general | solution.py:83
  269.8 18.5 %all-to-all-done.1 = bf16[8,448,256]{2,1,0:T(8,128)(2,1)S(1)} async-done(((bf16[8,448,256]{2,1,0:T(8,128)(2,1)}), bf16[8,448,256]{2,1,0:T(8,128)(2,1)S(1)}, u32[]{:S(2)}, u32[]{:S(2)}) %all-to-all-start.1) | async-done | bytes 1835040 | tf_op jit(solution)/shard_map/all_to_all | solution.py:32
  288.3 1.0 reduce_sum.43
Async XLA Ops:
  0.6 4.8 %copy-start = (bf16[128,3584]{1,0:T(8,128)(2,1)S(1)}, bf16[128,3584]{1,0:T(8,128)(2,1)}, u32[]{:S(2)}) copy-start(bf16[128,3584]{1,0:T(8,128)(2,1)} %param.6) | copy-start | bytes 2752516
  10.4 219.5 %copy-start.2 = (bf16[448,256]{1,0:T(8,128)(2,1)S(1)}, bf16[448,256]{1,0:T(8,128)(2,1)}, u32[]{:S(2)}) copy-start(bf16[448,256]{1,0:T(8,128)(2,1)} %param.11) | copy-start | bytes 688132
  231.3 27.9 %all-to-all-start.2 = ((bf16[8,448,256]{2,1,0:T(8,128)(2,1)}), bf16[8,448,256]{2,1,0:T(8,128)(2,1)S(1)}, u32[]{:S(2)}, u32[]{:S(2)}) async-start(bf16[8,448,256]{2,1,0:T(8,128)(2,1)} %broadcast_in_dim.8), calls=%async_computation.2 | async-start | bytes 3670016 | tf_op jit(solution)/shard_map/all_to_all | solution.py:11
  234.9 9.5 %copy-start.3 = (bf16[768,256]{1,0:T(8,128)(2,1)S(1)}, bf16[768,256]{1,0:T(8,128)(2,1)}, u32[]{:S(2)}) copy-start(bf16[768,256]{1,0:T(8,128)(2,1)} %param.10) | copy-start | bytes 1179652
  234.9 9.4 %copy-start.4 = (bf16[768,256]{1,0:T(8,128)(2,1)S(1)}, bf16[768,256]{1,0:T(8,128)(2,1)}, u32[]{:S(2)}) copy-start(bf16[768,256]{1,0:T(8,128)(2,1)} %param.9) | copy-start | bytes 1179652
  259.2 1.2 copy-start.1
  260.4 27.9 %all-to-all-start.1 = ((bf16[8,448,256]{2,1,0:T(8,128)(2,1)}), bf16[8,448,256]{2,1,0:T(8,128)(2,1)S(1)}, u32[]{:S(2)}, u32[]{:S(2)}) async-start(bf16[8,448,256]{2,1,0:T(8,128)(2,1)} %bitcast.17), calls=%async_computation.1 | async-start | bytes 3670016 | tf_op jit(solution)/shard_map/all_to_all | solution.py:32
where the time goes:
time: 290 us; the launch traced here: 289 us
  blocking collectives  220 us (76%)
  waiting for transfers between devices  27.8 us (10%)
  local copies, waits for them, and re-layouts  15.3 us (5%)
  matrix products  13 us (4%)
  starting transfers between devices  7.18 us (2%)
  other arithmetic  5.79 us (2%)
    all_to_all x1, blocking collectives, per_device(): lax.all_to_all(copies.reshape(devices, capacity, width), 'expert', split_...  220 us
    all_to_all x1, waiting for transfers between devices, sum_at_owner(): lax.all_to_all(parts, axis, split_axis=0, concat_axis=0, tiled=True)  18.5 us
    reshape x1, local copies, waits for them, and re-layouts, per_device(): routed = arrived.reshape(devices * capacity, width)  9.43 us
    all_to_all x1, waiting for transfers between devices, sent_to_all(): return lax.all_to_all(copies, axis, split_axis=0, concat_axis=0, tiled=True)  9.25 us
  transfers between devices with their start and end apart: 2, of which 2 were waited for; matrix products, arithmetic and copies ran while one was open for 7% of the time, Pallas kernels for 0%

commit v1 on v0

v1 whole, which is shorter than its diff:
```python
import jax
import jax.numpy as jnp
from jax import lax
from jax.sharding import PartitionSpec as P

SPLIT = 4


def slot_buffer(cotangent, expert_ids, route_weights, experts, capacity):
    columns = lax.broadcasted_iota(jnp.int32, (1, 1, experts), 2)
    onehot = (expert_ids[:, :, None] == columns).astype(jnp.int32)
    touched = jnp.sum(onehot, axis=1)
    earlier = jnp.cumsum(touched, axis=0) - touched
    position = jnp.sum(onehot * earlier[:, None, :], axis=2)
    target = expert_ids * capacity + position
    places = lax.broadcasted_iota(jnp.int32, (1, 1, experts * capacity), 2)
    chosen = (target[:, :, None] == places).astype(jnp.float32)
    picker = jnp.sum(chosen, axis=1)
    slot_scale = jnp.sum(chosen * route_weights[:, :, None], axis=(0, 1))
    picked = lax.dot_general(
        picker.astype(jnp.bfloat16),
        cotangent,
        (((0,), (0,)), ((), ())),
        preferred_element_type=jnp.float32,
    )
    return (picked * slot_scale[:, None]).astype(jnp.bfloat16)


def per_device(cotangent, expert_ids, route_weights, gate_pre, up_pre, down_weight):
    devices = lax.axis_size("expert")
    groups = lax.axis_size("dp")
    experts = devices // SPLIT
    rows, hidden = gate_pre.shape
    capacity = rows // devices
    width = cotangent.shape[1]
    part = width // SPLIT
    piece = part // groups
    quads = [[x * SPLIT + q for q in range(SPLIT)] for x in range(experts)]

    def quad_exchange(array):
        return lax.all_to_all(
            array, "expert", split_axis=0, concat_axis=0, axis_index_groups=quads, tiled=True
        )

    gate = gate_pre.astype(jnp.float32)
    up = up_pre.astype(jnp.float32)
    sigmoid = jax.nn.sigmoid(gate)
    active = gate * sigmoid
    product = (active * up).astype(jnp.bfloat16)

    ordered = cotangent.reshape(-1, groups, SPLIT, piece).transpose(0, 2, 1, 3).reshape(-1, width)
    buffer = slot_buffer(ordered, expert_ids, route_weights, experts, capacity)
    sent = buffer.reshape(experts, capacity // 4, 4, SPLIT, part).transpose(0, 3, 1, 2, 4)
    arrived = lax.all_to_all(
        sent.reshape(devices, capacity // 4, 4, part),
        "expert",
        split_axis=0,
        concat_axis=0,
        tiled=True,
    )
    routed = arrived.reshape(rows, part)

    weight = quad_exchange(down_weight.reshape(SPLIT, piece, hidden))
    weight = lax.all_to_all(
        jnp.broadcast_to(weight, (groups, *weight.shape)), "dp", split_axis=0, concat_axis=0, tiled=True
    )
    weight = weight.transpose(1, 0, 2, 3).reshape(SPLIT, part, hidden)
    products = quad_exchange(jnp.broadcast_to(product, (SPLIT, *product.shape)))

    partial = jnp.einsum("rd,jdf->jrf", routed, weight, preferred_element_type=jnp.float32)
    shares = quad_exchange(partial.astype(jnp.bfloat16))
    upstream = shares.astype(jnp.float32).sum(axis=0)
    gate_grad = (upstream * up * sigmoid * (1.0 + gate * (1.0 - sigmoid))).astype(jnp.bfloat16)
    up_grad = (upstream * active).astype(jnp.bfloat16)

    grads = jnp.einsum("rd,jrf->djf", routed, products, preferred_element_type=jnp.float32)
    grads = grads.astype(jnp.bfloat16).reshape(groups, piece, SPLIT, hidden)
    grads = lax.all_to_all(grads, "dp", split_axis=0, concat_axis=0, tiled=True)
    total = grads.astype(jnp.float32).sum(axis=0).astype(jnp.bfloat16)
    weight_grad = quad_exchange(total.transpose(1, 0, 2)).reshape(SPLIT * piece, hidden)
    return (weight_grad, gate_grad, up_grad)


def solution(mesh):
    placed = (
        P(("dp", "expert"), None),
        P(("dp", "expert"), None),
        P(("dp", "expert"), None),
        P("dp", "expert"),
        P("dp", "expert"),
        P("dp", "expert"),
    )
    return jax.shard_map(
        per_device,
        mesh=mesh,
        in_specs=placed,
        out_specs=(P("dp", "expert"), P("dp", "expert"), P("dp", "expert")),
        check_vma=False,
    )
```

time: 290 us -> 224 us (0.77)
  the two profiles are of different devices: /device:TPU:40 before, /device:TPU:1 now
where the time goes in v1:
time: 224 us; the launch traced here: 221 us
  blocking collectives  87.9 us (39%)
  waiting for transfers between devices  81.8 us (37%)
  starting transfers between devices  24.8 us (11%)
  local copies, waits for them, and re-layouts  14.2 us (6%)
  matrix products  6.6 us (3%)
  other arithmetic  4.63 us (2%)
    all_to_all x3, blocking collectives, quad_exchange(): lax.all_to_all(array, 'expert', split_axis=0, concat_axis=0, axis_index_g...  60.7 us
    all_to_all x1, waiting for transfers between devices, quad_exchange(): lax.all_to_all(array, 'expert', split_axis=0, concat_axis=0, axis_index_g...  35.2 us
    all_to_all x1, waiting for transfers between devices, per_device(): lax.all_to_all(sent.reshape(devices, capacity // 4, 4, part), 'expert', s...  32.4 us
    all_to_all x1, blocking collectives, per_device(): grads = lax.all_to_all(grads, 'dp', split_axis=0, concat_axis=0, tiled=True)  27.2 us
    all_to_all x1, waiting for transfers between devices, per_device(): lax.all_to_all(jnp.broadcast_to(weight, (groups, *weight.shape)), 'dp', s...  14.2 us
    all_to_all x1, starting transfers between devices, per_device(): lax.all_to_all(sent.reshape(devices, capacity // 4, 4, part), 'expert', s...  13.6 us
    all_to_all x1, starting transfers between devices, per_device(): lax.all_to_all(jnp.broadcast_to(weight, (groups, *weight.shape)), 'dp', s...  7.66 us
  transfers between devices with their start and end apart: 3, of which 3 were waited for; matrix products, arithmetic and copies ran while one was open for 5% of the time, Pallas kernels for 0%

profile of v1, /device:TPU:1, one launch (start us, length us, event | category | flops | bytes accessed | tf_op | source)
XLA Modules:
  0.0 220.6 jit_solution(6122382750011416665)
XLA Ops:
  0.6 13.6 %all_to_all.35 = bf16[4,112,256]{2,1,0:T(8,128)(2,1)S(1)} all-to-all(bf16[4,112,256]{2,1,0:T(8,128)(2,1)} %bitcast.41), channel_id=1, replica_groups={{0,1,2,3},{4,5,6,7},{8,9,10,11},{12,13,14,15},{16,17,18,19},{20,21,22,2..., dimensions={0} | all-to-all | bytes 458752 | tf_op jit(solution)/shard_map/all_to_all | solution.py:41
  14.2 1.4 broadcast_in_dim.5
  15.6 7.7 %all-to-all-start.5 = ((bf16[8,4,112,256]{3,2,1,0:T(8,128)(2,1)}), bf16[8,4,112,256]{3,2,1,0:T(8,128)(2,1)S(1)}, u32[]{:S(2)}, u32[]{:S(2)}) async-start(bf16[8,4,112,256]{3,2,1,0:T(8,128)(2,1)} %broadcast_in_dim.5), calls=%async_computation.5 | async-start | bytes 3670016 | tf_op jit(solution)/shard_map/all_to_all | solution.py:64
  23.3 0.0 copy-start.4
  23.3 0.0 copy-start.3
  23.3 1.6 copy.20
  24.8 0.1 copy.21
  24.9 0.0 copy-done.4
  24.9 2.6 %fusion.18 = s32[128]{0:T(128)S(1)} fusion(s32[128]{0:T(128)S(1)} %bitcast.43), kind=kOutput, calls=%fused_computation.34 | output fusion | flops 274304 | bytes 1024 | tf_op jit(solution)/shard_map/jit(cumsum)/reduce_window_sum | solution.py:13
  27.6 0.0 copy-done.3
  27.6 0.1 select_reduce_fusion
  27.7 0.5 fusion
  28.2 1.3 reshape.248
  29.5 3.0 %copy.22 = bf16[16,3,4,4,896]{4,2,1,3,0:T(4,128)(2,1)} copy(bf16[16,3,4,4,896]{4,3,2,1,0:T(4,128)(2,1)} %reshape.248) | data formatting | bytes 2752512 | tf_op jit(solution)/shard_map/reshape | solution.py:53
  32.5 14.2 %all-to-all-done.5 = bf16[8,4,112,256]{3,2,1,0:T(8,128)(2,1)S(1)} async-done(((bf16[8,4,112,256]{3,2,1,0:T(8,128)(2,1)}), bf16[8,4,112,256]{3,2,1,0:T(8,128)(2,1)S(1)}, u32[]{:S(2)}, u32[]{:S(2)}) %all-to-all-start.5) | async-done | bytes 1835040 | tf_op jit(solution)/shard_map/all_to_all | solution.py:64
  46.7 13.6 %all-to-all-start = ((bf16[64,3,4,896]{3,2,1,0:T(4,128)(2,1)}), bf16[64,3,4,896]{3,2,1,0:T(4,128)(2,1)S(1)}, u32[]{:S(2)}, u32[]{:S(2)}) async-start(bf16[64,3,4,896]{3,2,1,0:T(4,128)(2,1)} %bitcast.34), calls=%async_computation | async-start | bytes 2752512 | tf_op jit(solution)/shard_map/all_to_all | solution.py:54
  60.2 1.4 copy.25
  61.6 0.0 copy-start
  61.6 32.4 %all-to-all-done = bf16[64,3,4,896]{3,2,1,0:T(4,128)(2,1)S(1)} async-done(((bf16[64,3,4,896]{3,2,1,0:T(4,128)(2,1)}), bf16[64,3,4,896]{3,2,1,0:T(4,128)(2,1)S(1)}, u32[]{:S(2)}, u32[]{:S(2)}) %all-to-all-start) | async-done | bytes 1376288 | tf_op jit(solution)/shard_map/all_to_all | solution.py:54
  94.1 1.3 reshape.256
  95.3 0.0 copy-done
  95.3 3.1 %fusion.1 = bf16[4,768,256]{2,1,0:T(8,128)(2,1)S(1)} fusion(bf16[768,896,1]{1,0,2:T(8,128)(2,1)} %reshape.256, bf16[4,896,256]{2,1,0:T(8,128)(2,1)S(1)} %bitcast.37), kind=kOutput, calls=%fused_computation.5 | convolution fusion | flops 1410072576 | bytes 4784128 | tf_op jit(solution)/shard_map/rd,jdf->jrf/dot_general | solution.py:70
  98.5 39.0 %all_to_all.36 = bf16[4,768,256]{2,1,0:T(8,128)(2,1)S(1)} all-to-all(bf16[4,768,256]{2,1,0:T(8,128)(2,1)S(1)} %fusion.1), channel_id=1, replica_groups={{0,1,2,3},{4,5,6,7},{8,9,10,11},{12,13,14,15},{16,17,18,19},{20,21,22,2..., dimensions={0} | all-to-all | bytes 3145728 | tf_op jit(solution)/shard_map/all_to_all | solution.py:41
  137.5 0.0 copy-start.1
  137.5 0.0 copy-start.2
  137.5 0.2 convert_reduce_fusion
  137.7 0.7 copy-done.1
  138.5 0.1 copy-done.2
  138.6 1.3 multiply_convert_fusion
  139.9 1.3 broadcast_in_dim.4
  141.2 3.6 %all-to-all-start.1 = ((bf16[4,768,256]{2,1,0:T(8,128)(2,1)}), bf16[4,768,256]{2,1,0:T(8,128)(2,1)S(1)}, u32[]{:S(2)}, u32[]{:S(2)}) async-start(bf16[4,768,256]{2,1,0:T(8,128)(2,1)} %broadcast_in_dim.4), calls=%async_computation.1 | async-start | bytes 3145728 | tf_op jit(solution)/shard_map/all_to_all | solution.py:41
  144.7 1.3 reshape.250
  146.0 35.2 %all-to-all-done.1 = bf16[4,768,256]{2,1,0:T(8,128)(2,1)S(1)} async-done(((bf16[4,768,256]{2,1,0:T(8,128)(2,1)}), bf16[4,768,256]{2,1,0:T(8,128)(2,1)S(1)}, u32[]{:S(2)}, u32[]{:S(2)}) %all-to-all-start.1) | async-done | bytes 1572896 | tf_op jit(solution)/shard_map/all_to_all | solution.py:41
  181.2 3.0 %convolution_convert_fusion = bf16[896,4,256]{2,0,1:T(8,128)(2,1)S(1)} fusion(bf16[4,768,256]{2,1,0:T(8,128)(2,1)S(1)} %all-to-all-done.1, bf16[768,896]{1,0:T(8,128)(2,1)} %reshape.250), kind=kOutput, calls=%fused_computation.3 | convolution fusion | flops 1410203648 | bytes 4784128 | tf_op jit(solution)/shard_map/rd,jrf->djf/dot_general | solution.py:76
  184.2 0.1 copy.24
  184.3 27.2 %all_to_all.37 = bf16[8,112,4,256]{3,1,2,0:T(8,128)(2,1)S(1)} all-to-all(bf16[8,112,4,256]{3,1,2,0:T(8,128)(2,1)S(1)} %copy.24), channel_id=1, replica_groups=mesh['dp'=8,'expert'=64] {'dp'}, dimensions={0} | all-to-all | bytes 3670016 | tf_op jit(solution)/shard_map/all_to_all | solution.py:78
  211.5 0.3 reduce_sum.52
  211.8 8.1 %all_to_all.38 = bf16[4,112,256]{2,1,0:T(8,128)(2,1)S(1)} all-to-all(bf16[4,112,256]{2,1,0:T(8,128)(2,1)S(1)} %bitcast.39), channel_id=1, replica_groups={{0,1,2,3},{4,5,6,7},{8,9,10,11},{12,13,14,15},{16,17,18,19},{20,21,22,2..., dimensions={0} | all-to-all | bytes 458752 | tf_op jit(solution)/shard_map/all_to_all | solution.py:41
  219.9 0.7 copy.29
  (1 shorter events, 0.0 us)
Async XLA Ops:
  15.6 31.1 %all-to-all-start.5 = ((bf16[8,4,112,256]{3,2,1,0:T(8,128)(2,1)}), bf16[8,4,112,256]{3,2,1,0:T(8,128)(2,1)S(1)}, u32[]{:S(2)}, u32[]{:S(2)}) async-start(bf16[8,4,112,256]{3,2,1,0:T(8,128)(2,1)} %broadcast_in_dim.5), calls=%async_computation.5 | async-start | bytes 3670016 | tf_op jit(solution)/shard_map/all_to_all | solution.py:64
  23.3 1.7 copy-start.4
  23.3 4.3 %copy-start.3 = (f32[128,1]{0,1:T(1,128)S(1)}, f32[128,1]{0,1:T(1,128)}, u32[]{:S(2)}) copy-start(f32[128,1]{0,1:T(1,128)} %param.8) | copy-start | bytes 1540
  46.7 47.4 %all-to-all-start = ((bf16[64,3,4,896]{3,2,1,0:T(4,128)(2,1)}), bf16[64,3,4,896]{3,2,1,0:T(4,128)(2,1)S(1)}, u32[]{:S(2)}, u32[]{:S(2)}) async-start(bf16[64,3,4,896]{3,2,1,0:T(4,128)(2,1)} %bitcast.34), calls=%async_computation | async-start | bytes 2752512 | tf_op jit(solution)/shard_map/all_to_all | solution.py:54
  61.6 33.7 %copy-start = (bf16[4,8,112,256]{3,2,1,0:T(8,128)(2,1)S(1)}, bf16[4,8,112,256]{3,2,1,0:T(8,128)(2,1)}, u32[]{:S(2)}) copy-start(bf16[4,8,112,256]{3,2,1,0:T(8,128)(2,1)} %copy.25) | copy-start | bytes 5505028
  137.5 1.0 copy-start.1
  137.5 1.1 copy-start.2
  141.2 40.1 %all-to-all-start.1 = ((bf16[4,768,256]{2,1,0:T(8,128)(2,1)}), bf16[4,768,256]{2,1,0:T(8,128)(2,1)S(1)}, u32[]{:S(2)}, u32[]{:S(2)}) async-start(bf16[4,768,256]{2,1,0:T(8,128)(2,1)} %broadcast_in_dim.4), calls=%async_computation.1 | async-start | bytes 3145728 | tf_op jit(solution)/shard_map/all_to_all | solution.py:41

commit v2 on v1

v2 whole, which is shorter than its diff:
```python
import functools

import jax
import jax.numpy as jnp
from jax import lax
from jax.experimental import pallas as pl
from jax.experimental.pallas import tpu as pltpu
from jax.sharding import PartitionSpec as P

SPLIT = 4
MESH = pl.DeviceIdType.MESH


def slot_buffer(cotangent, expert_ids, route_weights, experts, capacity):
    columns = lax.broadcasted_iota(jnp.int32, (1, 1, experts), 2)
    onehot = (expert_ids[:, :, None] == columns).astype(jnp.int32)
    touched = jnp.sum(onehot, axis=1)
    earlier = jnp.cumsum(touched, axis=0) - touched
    position = jnp.sum(onehot * earlier[:, None, :], axis=2)
    target = expert_ids * capacity + position
    places = lax.broadcasted_iota(jnp.int32, (1, 1, experts * capacity), 2)
    chosen = (target[:, :, None] == places).astype(jnp.float32)
    picker = jnp.sum(chosen, axis=1)
    slot_scale = jnp.sum(chosen * route_weights[:, :, None], axis=(0, 1))
    picked = lax.dot_general(
        picker.astype(jnp.bfloat16),
        cotangent,
        (((0,), (0,)), ((), ())),
        preferred_element_type=jnp.float32,
    )
    return (picked * slot_scale[:, None]).astype(jnp.bfloat16)


def wait_bytes(ref, sem):
    pltpu.make_async_copy(ref, ref, sem).wait()


def layer_kernel(
    dims,
    sent,
    gate,
    up,
    down,
    weight_grad,
    gate_grad,
    up_grad,
    arrived,
    routed,
    own_weight,
    weight,
    products,
    partial,
    shares,
    grads,
    grad_parts,
    total,
    grad_rows,
    send_sems,
    token_sems,
    quad_weight_sems,
    weight_sems,
    product_sems,
    share_sems,
    grad_sems,
    total_sems,
):
    groups, devices, ring = dims
    rows_y = devices // ring
    rows, hidden = gate.shape
    capacity = rows // devices
    chunk = rows // rows_y
    piece = down.shape[0] // SPLIT
    part = piece * groups
    i = lax.axis_index("dp")
    e = lax.axis_index("expert")
    y, z = e // ring, e % ring
    q = e % SPLIT
    base = e - q

    def peer(target):
        return {"expert": target}

    barrier = pltpu.get_barrier_semaphore()

    @pl.loop(1, devices)
    def _(step):
        target = lax.rem(e + step, devices)
        pl.semaphore_signal(barrier, inc=1, device_id=peer(target), device_id_type=MESH)

    @pl.loop(1, groups)
    def _(step):
        target = lax.rem(i + step, groups)
        pl.semaphore_signal(barrier, inc=1, device_id={"dp": target}, device_id_type=MESH)

    arrived[e] = sent[e]
    own_weight[q] = down[pl.ds(pl.multiple_of(q * piece, 16), piece), :]
    pl.semaphore_wait(barrier, devices - 1 + groups - 1)

    for step in range(1, SPLIT):
        other = lax.rem(q + step, SPLIT)
        pltpu.make_async_remote_copy(
            src_ref=down.at[pl.ds(pl.multiple_of(other * piece, 16), piece)],
            dst_ref=own_weight.at[q],
            send_sem=send_sems.at[0],
            recv_sem=quad_weight_sems.at[q],
            device_id=peer(base + other),
            device_id_type=MESH,
        ).start()

    def away(step, count):
        return jnp.where(step % 2 == 1, (step + 1) // 2, count - step // 2)

    @pl.loop(0, devices)
    def _(step):
        to_y = lax.rem(y + away(step // ring, rows_y), rows_y)
        to_z = lax.rem(z + away(step % ring, ring), ring)
        target = to_y * ring + to_z

        @pl.when(target != e)
        def _():
            pltpu.make_async_remote_copy(
                src_ref=sent.at[target],
                dst_ref=arrived.at[e],
                send_sem=send_sems.at[1],
                recv_sem=token_sems.at[e],
                device_id=peer(target),
                device_id_type=MESH,
            ).start()

    @pl.loop(0, rows_y)
    def _(step):
        span = pl.ds(pl.multiple_of(step * chunk, 16), chunk)
        g = gate[span, :].astype(jnp.float32)
        active = g / (1.0 + jnp.exp(-g))
        products[q, span, :] = (active * up[span, :].astype(jnp.float32)).astype(jnp.bfloat16)

    for step in range(1, SPLIT):
        other = lax.rem(q + step, SPLIT)
        wait_bytes(own_weight.at[other], quad_weight_sems.at[other])
    weight[i] = own_weight[...]

    @pl.loop(1, groups)
    def _(step):
        target = lax.rem(i + step, groups)
        pltpu.make_async_remote_copy(
            src_ref=own_weight,
            dst_ref=weight.at[i],
            send_sem=send_sems.at[2],
            recv_sem=weight_sems.at[i],
            device_id={"dp": target},
            device_id_type=MESH,
        ).start()

    for step in range(1, SPLIT):
        other = lax.rem(q + step, SPLIT)
        pltpu.make_async_remote_copy(
            src_ref=products.at[q],
            dst_ref=products.at[q],
            send_sem=send_sems.at[3],
            recv_sem=product_sems.at[q],
            device_id=peer(base + other),
            device_id_type=MESH,
        ).start()

    @pl.loop(1, groups)
    def _(step):
        source = lax.rem(i + step, groups)
        wait_bytes(weight.at[source], weight_sems.at[source])

    @pl.loop(0, rows_y)
    def _(step):
        from_y = lax.rem(y + rows_y - lax.rem(away(step, rows_y), rows_y), rows_y)

        @pl.loop(0, ring)
        def _(at):
            source = from_y * ring + at

            @pl.when(source != e)
            def _():
                wait_bytes(arrived.at[source], token_sems.at[source])

        block = arrived[pl.ds(from_y * ring, ring)].reshape(chunk, part)
        span = pl.ds(pl.multiple_of(from_y * chunk, 16), chunk)
        routed[span, :] = block
        for j in range(SPLIT):
            partial[j, span, :] = jnp.dot(
                block, weight[:, j].reshape(part, hidden), preferred_element_type=jnp.float32
            ).astype(jnp.bfloat16)
        shares[q, span, :] = partial[q, span, :]
        for hop in range(1, SPLIT):
            other = lax.rem(q + hop, SPLIT)
            pltpu.make_async_remote_copy(
                src_ref=partial.at[other, span],
                dst_ref=shares.at[q, span],
                send_sem=send_sems.at[4],
                recv_sem=share_sems.at[q, from_y],
                device_id=peer(base + other),
                device_id_type=MESH,
            ).start()

    for step in range(1, SPLIT):
        other = lax.rem(q + step, SPLIT)
        wait_bytes(products.at[other], product_sems.at[other])

    @pl.loop(0, SPLIT)
    def _(j):
        grads[:, j] = (
            lax.dot_general(
                routed[...],
                products[j],
                (((0,), (0,)), ((), ())),
                preferred_element_type=jnp.float32,
            )
            .astype(jnp.bfloat16)
            .reshape(groups, piece, hidden)
        )

    grad_parts[i] = grads[i]

    @pl.loop(1, groups)
    def _(step):
        target = lax.rem(i + step, groups)
        pltpu.make_async_remote_copy(
            src_ref=grads.at[target],
            dst_ref=grad_parts.at[i],
            send_sem=send_sems.at[5],
            recv_sem=grad_sems.at[i],
            device_id={"dp": target},
            device_id_type=MESH,
        ).start()

    @pl.loop(0, rows_y)
    def _(step):
        from_y = lax.rem(y + rows_y - lax.rem(away(step, rows_y), rows_y), rows_y)
        span = pl.ds(pl.multiple_of(from_y * chunk, 16), chunk)
        for hop in range(1, SPLIT):
            other = lax.rem(q + hop, SPLIT)
            wait_bytes(shares.at[other, span], share_sems.at[other, from_y])
        upstream = shares[0, span, :].astype(jnp.float32)
        for j in range(1, SPLIT):
            upstream = upstream + shares[j, span, :].astype(jnp.float32)
        g = gate[span, :].astype(jnp.float32)
        u = up[span, :].astype(jnp.float32)
        sigmoid = 1.0 / (1.0 + jnp.exp(-g))
        gate_grad[span, :] = (upstream * u * sigmoid * (1.0 + g * (1.0 - sigmoid))).astype(
            jnp.bfloat16
        )
        up_grad[span, :] = (upstream * (g * sigmoid)).astype(jnp.bfloat16)

    @pl.loop(1, groups)
    def _(step):
        source = lax.rem(i + step, groups)
        wait_bytes(grad_parts.at[source], grad_sems.at[source])

    @pl.loop(0, SPLIT)
    def _(j):
        whole = grad_parts[0, j].astype(jnp.float32)
        for k in range(1, groups):
            whole = whole + grad_parts[k, j].astype(jnp.float32)
        total[j] = whole.astype(jnp.bfloat16)

    grad_rows[q] = total[q]
    for step in range(1, SPLIT):
        other = lax.rem(q + step, SPLIT)
        pltpu.make_async_remote_copy(
            src_ref=total.at[other],
            dst_ref=grad_rows.at[q],
            send_sem=send_sems.at[6],
            recv_sem=total_sems.at[q],
            device_id=peer(base + other),
            device_id_type=MESH,
        ).start()
    for step in range(1, SPLIT):
        other = lax.rem(q + step, SPLIT)
        wait_bytes(grad_rows.at[other], total_sems.at[other])
    for j in range(SPLIT):
        weight_grad[j * piece : (j + 1) * piece, :] = grad_rows[j]

    wait_bytes(own_weight.at[pl.ds(0, SPLIT - 1)], send_sems.at[0])
    wait_bytes(arrived.at[pl.ds(0, devices - 1)], send_sems.at[1])
    wait_bytes(weight.at[pl.ds(0, groups - 1)], send_sems.at[2])
    wait_bytes(products.at[pl.ds(0, SPLIT - 1)], send_sems.at[3])
    wait_bytes(shares.at[pl.ds(0, SPLIT - 1)], send_sems.at[4])
    wait_bytes(grads.at[pl.ds(0, groups - 1)], send_sems.at[5])
    wait_bytes(total.at[pl.ds(0, SPLIT - 1)], send_sems.at[6])


def per_device(cotangent, expert_ids, route_weights, gate_pre, up_pre, down_weight):
    devices = lax.axis_size("expert")
    groups = lax.axis_size("dp")
    ring = 8 if devices == 64 else SPLIT
    experts = devices // SPLIT
    rows, hidden = gate_pre.shape
    capacity = rows // devices
    width = cotangent.shape[1]
    part = width // SPLIT
    piece = part // groups

    ordered = cotangent.reshape(-1, groups, SPLIT, piece).transpose(0, 2, 1, 3).reshape(-1, width)
    buffer = slot_buffer(ordered, expert_ids, route_weights, experts, capacity)
    sent = buffer.reshape(experts, capacity // 4, 4, SPLIT, part).transpose(0, 3, 1, 2, 4)
    sent = sent.reshape(devices, capacity // 4, 4, part)

    half = jnp.bfloat16
    vmem = pl.BlockSpec(memory_space=pltpu.VMEM)
    dma = pltpu.SemaphoreType.DMA
    return pl.pallas_call(
        functools.partial(layer_kernel, (groups, devices, ring)),
        out_shape=(
            jax.ShapeDtypeStruct(down_weight.shape, half),
            jax.ShapeDtypeStruct(gate_pre.shape, half),
            jax.ShapeDtypeStruct(gate_pre.shape, half),
        ),
        in_specs=[vmem] * 4,
        out_specs=(vmem, vmem, vmem),
        scratch_shapes=[
            pltpu.VMEM((devices, capacity // 4, 4, part), half),
            pltpu.VMEM((rows, part), half),
            pltpu.VMEM((SPLIT, piece, hidden), half),
            pltpu.VMEM((groups, SPLIT, piece, hidden), half),
            pltpu.VMEM((SPLIT, rows, hidden), half),
            pltpu.VMEM((SPLIT, rows, hidden), half),
            pltpu.VMEM((SPLIT, rows, hidden), half),
            pltpu.VMEM((groups, SPLIT, piece, hidden), half),
            pltpu.VMEM((groups, SPLIT, piece, hidden), half),
            pltpu.VMEM((SPLIT, piece, hidden), half),
            pltpu.VMEM((SPLIT, piece, hidden), half),
            dma((7,)),
            dma((devices,)),
            dma((SPLIT,)),
            dma((groups,)),
            dma((SPLIT,)),
            dma((SPLIT, devices // ring)),
            dma((groups,)),
            dma((SPLIT,)),
        ],
        compiler_params=pltpu.CompilerParams(
            collective_id=0, has_side_effects=True, vmem_limit_bytes=48 * 1024 * 1024
        ),
    )(sent, gate_pre, up_pre, down_weight)


def solution(mesh):
    placed = (
        P(("dp", "expert"), None),
        P(("dp", "expert"), None),
        P(("dp", "expert"), None),
        P("dp", "expert"),
        P("dp", "expert"),
        P("dp", "expert"),
    )
    return jax.shard_map(
        per_device,
        mesh=mesh,
        in_specs=placed,
        out_specs=(P("dp", "expert"), P("dp", "expert"), P("dp", "expert")),
        check_vma=False,
    )
```

time: 224 us -> 145 us (0.65); the launches traced: 221 us -> 145 us
  Pallas kernels: 0 us -> 134 us
  blocking collectives: 87.9 us -> 0 us
  waiting for transfers between devices: 81.8 us -> 0 us
  starting transfers between devices: 24.8 us -> 0 us
  local copies, waits for them, and re-layouts: 14.2 us -> 5.3 us
  matrix products: 6.6 us -> 0.52 us
    pallas_call x0 -> x1, Pallas kernels: none -> 134 us  [per_device(): pl.pallas_call(functools.partial(layer_kernel, (groups, devices, ring)),...]
    all_to_all x4 -> x0, blocking collectives: 87.9 us -> none  [the longest x3 60.7 us: quad_exchange(): lax.all_to_all(array, 'expert', split_axis=0, concat_axis=0, axis_index_g...]
    all_to_all x3 -> x0, waiting for transfers between devices: 81.8 us -> none  [the longest x1 35.2 us: quad_exchange(): lax.all_to_all(array, 'expert', split_axis=0, concat_axis=0, axis_index_g...]
    all_to_all x3 -> x0, starting transfers between devices: 24.8 us -> none  [the longest x1 13.6 us: per_device(): lax.all_to_all(sent.reshape(devices, capacity // 4, 4, part), 'expert', s...]
    dot_general x2 -> x0, matrix products: 6.08 us -> none  [the longest x1 3.12 us: per_device(): jnp.einsum('rd,jdf->jrf', routed, weight, preferred_element_type=jnp.floa...]
    reshape x2, local copies, waits for them, and re-layouts: 4.23 us -> 0.89 us  [per_device(): buffer.reshape(experts, capacity // 4, 4, SPLIT, part)]
    reshape x3 -> x0, local copies, waits for them, and re-layouts: 2.67 us -> none  [the longest x2 2.52 us: per_device(): routed = arrived.reshape(rows, part)]
    broadcast_in_dim x2 -> x0, local copies, waits for them, and re-layouts: 2.66 us -> none  [the longest x1 1.4 us: per_device(): jnp.broadcast_to(weight, (groups, *weight.shape))]
  transfers between devices with their start and end apart: 3 -> 0, of which waited for: 3 -> 0; matrix products, arithmetic and copies ran while one was open for 5% -> 0% of each run, Pallas kernels for 0% -> 0%
where the time goes in v2:
time: 145 us
  Pallas kernels  134 us (92%)
  local copies, waits for them, and re-layouts  5.3 us (4%)
  other arithmetic  4.79 us (3%)
    pallas_call x1, Pallas kernels, per_device(): pl.pallas_call(functools.partial(layer_kernel, (groups, devices, ring)),...  134 us
    unnamed x10, local copies, waits for them, and re-layouts  4.35 us
    another operation x1, other arithmetic, slot_buffer(): earlier = jnp.cumsum(touched, axis=0) - touched  3.36 us

profile of v2, /device:TPU:1, one launch (start us, length us, event | category | flops | bytes accessed | tf_op | source)
XLA Modules:
  0.0 145.2 jit_solution(15163650251517680786)
XLA Ops:
  0.6 3.4 %fusion.8 = s32[128]{0:T(128)S(1)} fusion(s32[128]{0:T(128)} %bitcast.23), kind=kOutput, calls=%fused_computation.15 | output fusion | flops 274304 | bytes 1024 | tf_op jit(solution)/shard_map/jit(cumsum)/reduce_window_sum | solution.py:18
  4.0 0.7 fusion.7
  4.7 0.8 select_reduce_fusion
  5.4 1.6 %copy.13 = bf16[128,3584]{0,1:T(8,128)(2,1)S(1)} copy(bf16[128,3584]{1,0:T(8,128)(2,1)} %param.6) | data formatting | bytes 1835008 | tf_op args[0]
  7.0 0.1 copy.14
  7.1 0.5 fusion
  7.6 0.4 reshape.233
  8.0 0.0 copy-start
  8.0 0.0 copy-start.1
  8.0 0.0 copy-start.2
  8.0 0.5 copy.15
  8.5 0.4 copy-done
  9.0 0.1 copy-done.1
  9.1 0.1 copy-done.2
  9.1 133.8 %shard_map.91 = (bf16[448,256]{1,0:T(8,128)(2,1)S(1)}, bf16[768,256]{1,0:T(8,128)(2,1)S(1)}, bf16[768,256]{1,0:T(8,128)(2,1)S(1)}) custom-call(bf16[64,3,4,896]{3,2,1,0:T(4,128)(2,1)S(1)} %bitcast.19, bf16[768,256]{1,0:T(8,128)(2,1)S(1)} %copy-done, bf16[768,256]{1,0:T(8,128)(2,1)S(1)} %copy-done.1, bf16[448,256]{1,0:T(8,128)(2,1)S(1)} %copy-done.2), custom_call_target="tpu_custom_call" | custom-call | tf_op jit(solution)/shard_map/pallas_call | solution.py:307
  143.0 0.7 copy.19
  143.7 0.7 copy.20
  144.4 0.7 copy.21
Async XLA Ops:
  8.0 1.0 copy-start
  8.0 1.1 copy-start.1
  8.0 1.2 copy-start.2

commit v3 on v2

--- a/solution.py
+++ b/solution.py
@@ -8,27 +8,55 @@
 from jax.sharding import PartitionSpec as P
 
 SPLIT = 4
+PASS_ON = 2
 MESH = pl.DeviceIdType.MESH
 
 
-def slot_buffer(cotangent, expert_ids, route_weights, experts, capacity):
-    columns = lax.broadcasted_iota(jnp.int32, (1, 1, experts), 2)
-    onehot = (expert_ids[:, :, None] == columns).astype(jnp.int32)
-    touched = jnp.sum(onehot, axis=1)
-    earlier = jnp.cumsum(touched, axis=0) - touched
-    position = jnp.sum(onehot * earlier[:, None, :], axis=2)
-    target = expert_ids * capacity + position
-    places = lax.broadcasted_iota(jnp.int32, (1, 1, experts * capacity), 2)
-    chosen = (target[:, :, None] == places).astype(jnp.float32)
-    picker = jnp.sum(chosen, axis=1)
-    slot_scale = jnp.sum(chosen * route_weights[:, :, None], axis=(0, 1))
-    picked = lax.dot_general(
-        picker.astype(jnp.bfloat16),
-        cotangent,
-        (((0,), (0,)), ((), ())),
+def fill_slots(groups, cotangent, ids, scales, ordered, sent):
+    experts, _, quarters, lanes4, part = sent.shape
+    tokens, width = cotangent.shape
+    capacity = quarters * lanes4
+    piece = part // groups
+    lanes = 128 if part % 128 == 0 else part
+    at = lax.broadcasted_iota(jnp.int32, (tokens, lanes), 1)
+    for tile in range(width // lanes):
+        whole = None
+        lane = 0
+        while lane < lanes:
+            q, rest = divmod(tile * lanes + lane, part)
+            i, t = divmod(rest, piece)
+            source = i * SPLIT * piece + q * piece + t
+            run = min(lanes - lane, piece - t, lanes - source % lanes)
+            block = cotangent[:, source // lanes * lanes : (source // lanes + 1) * lanes]
+            block = block.astype(jnp.float32)
+            shift = (lane - source % lanes) % lanes
+            if shift:
+                block = pltpu.roll(block, shift, 1)
+            whole = block if whole is None else jnp.where(at >= lane, block, whole)
+            lane += run
+        q, rest = divmod(tile * lanes, part)
+        ordered[q, :, rest : rest + lanes] = whole.astype(jnp.bfloat16)
+
+    names = ids[...]
+    onehot = lax.broadcasted_iota(jnp.int32, (experts, tokens), 0) == names
+    onehot = onehot.astype(jnp.float32)
+    before = lax.broadcasted_iota(jnp.int32, (tokens, tokens), 0)
+    before = before < lax.broadcasted_iota(jnp.int32, (tokens, tokens), 1)
+    earlier = jnp.dot(
+        onehot.astype(jnp.bfloat16),
+        before.astype(jnp.float32).astype(jnp.bfloat16),
         preferred_element_type=jnp.float32,
     )
-    return (picked * slot_scale[:, None]).astype(jnp.bfloat16)
+    position = jnp.sum(onehot * earlier, axis=0, keepdims=True)
+    place = names.astype(jnp.float32) * capacity + position
+    slots = lax.broadcasted_iota(jnp.int32, (experts * capacity, tokens), 0)
+    picker = (slots.astype(jnp.float32) == place).astype(jnp.float32)
+    slot_scale = jnp.sum(picker * scales[...], axis=1, keepdims=True)
+    picker = picker.astype(jnp.bfloat16)
+    for q in range(SPLIT):
+        picked = jnp.dot(picker, ordered[q], preferred_element_type=jnp.float32)
+        picked = (picked * slot_scale).astype(jnp.bfloat16)
+        sent[:, q] = picked.reshape(experts, quarters, lanes4, part)
 
 
 def wait_bytes(ref, sem):
@@ -37,13 +65,17 @@
 
 def layer_kernel(
     dims,
-    sent,
+    cotangent,
+    ids,
+    scales,
     gate,
     up,
     down,
     weight_grad,
     gate_grad,
     up_grad,
+    ordered,
+    sent,
     arrived,
     routed,
     own_weight,
@@ -92,7 +124,16 @@
         target = lax.rem(i + step, groups)
         pl.semaphore_signal(barrier, inc=1, device_id={"dp": target}, device_id_type=MESH)
 
-    arrived[e] = sent[e]
+    fill_slots(groups, cotangent, ids, scales, ordered, sent)
+    arrived[e] = sent[e // SPLIT, q]
+
+    @pl.loop(0, rows_y)
+    def _(step):
+        span = pl.ds(pl.multiple_of(step * chunk, 16), chunk)
+        g = gate[span, :].astype(jnp.float32)
+        active = g / (1.0 + jnp.exp(-g))
+        products[q, span, :] = (active * up[span, :].astype(jnp.float32)).astype(jnp.bfloat16)
+
     own_weight[q] = down[pl.ds(pl.multiple_of(q * piece, 16), piece), :]
     pl.semaphore_wait(barrier, devices - 1 + groups - 1)
 
@@ -107,6 +148,26 @@
             device_id_type=MESH,
         ).start()
 
+    inner = (q == 1) | (q == 2)
+
+    def product_to(block, other, stage):
+        pltpu.make_async_remote_copy(
+            src_ref=products.at[block],
+            dst_ref=products.at[block],
+            send_sem=send_sems.at[stage],
+            recv_sem=product_sems.at[block],
+            device_id=peer(base + other),
+            device_id_type=MESH,
+        ).start()
+
+    @pl.when(q < SPLIT - 1)
+    def _():
+        product_to(q, q + 1, 3)
+
+    @pl.when(q > 0)
+    def _():
+        product_to(q, q - 1, 3)
+
     def away(step, count):
         return jnp.where(step % 2 == 1, (step + 1) // 2, count - step // 2)
 
@@ -119,20 +180,13 @@
         @pl.when(target != e)
         def _():
             pltpu.make_async_remote_copy(
-                src_ref=sent.at[target],
+                src_ref=sent.at[target // SPLIT, target % SPLIT],
                 dst_ref=arrived.at[e],
                 send_sem=send_sems.at[1],
                 recv_sem=token_sems.at[e],
                 device_id=peer(target),
                 device_id_type=MESH,
             ).start()
-
-    @pl.loop(0, rows_y)
-    def _(step):
-        span = pl.ds(pl.multiple_of(step * chunk, 16), chunk)
-        g = gate[span, :].astype(jnp.float32)
-        active = g / (1.0 + jnp.exp(-g))
-        products[q, span, :] = (active * up[span, :].astype(jnp.float32)).astype(jnp.bfloat16)
 
     for step in range(1, SPLIT):
         other = lax.rem(q + step, SPLIT)
@@ -151,17 +205,6 @@
             device_id_type=MESH,
         ).start()
 
-    for step in range(1, SPLIT):
-        other = lax.rem(q + step, SPLIT)
-        pltpu.make_async_remote_copy(
-            src_ref=products.at[q],
-            dst_ref=products.at[q],
-            send_sem=send_sems.at[3],
-            recv_sem=product_sems.at[q],
-            device_id=peer(base + other),
-            device_id_type=MESH,
-        ).start()
-
     @pl.loop(1, groups)
     def _(step):
         source = lax.rem(i + step, groups)
@@ -178,6 +221,12 @@
             @pl.when(source != e)
             def _():
                 wait_bytes(arrived.at[source], token_sems.at[source])
+
+        @pl.when(inner & (step == min(PASS_ON, rows_y - 1)))
+        def _():
+            for way in (1, -1):
+                wait_bytes(products.at[q - way], product_sems.at[q - way])
+                product_to(q - way, q + way, 7)
 
         block = arrived[pl.ds(from_y * ring, ring)].reshape(chunk, part)
         span = pl.ds(pl.multiple_of(from_y * chunk, 16), chunk)
@@ -198,9 +247,18 @@
                 device_id_type=MESH,
             ).start()
 
-    for step in range(1, SPLIT):
-        other = lax.rem(q + step, SPLIT)
-        wait_bytes(products.at[other], product_sems.at[other])
+    far = jnp.where(q == 1, SPLIT - 1, 0)
+
+    @pl.when(inner)
+    def _():
+        wait_bytes(products.at[far], product_sems.at[far])
+        product_to(far, jnp.where(q == 1, 0, SPLIT - 1), 8)
+
+    @pl.when(jnp.logical_not(inner))
+    def _():
+        for step in range(1, SPLIT):
+            other = lax.rem(q + step, SPLIT)
+            wait_bytes(products.at[other], product_sems.at[other])
 
     @pl.loop(0, SPLIT)
     def _(j):
@@ -279,7 +337,17 @@
     wait_bytes(own_weight.at[pl.ds(0, SPLIT - 1)], send_sems.at[0])
     wait_bytes(arrived.at[pl.ds(0, devices - 1)], send_sems.at[1])
     wait_bytes(weight.at[pl.ds(0, groups - 1)], send_sems.at[2])
-    wait_bytes(products.at[pl.ds(0, SPLIT - 1)], send_sems.at[3])
+
+    @pl.when(inner)
+    def _():
+        wait_bytes(products.at[pl.ds(0, 2)], send_sems.at[3])
+        wait_bytes(products.at[pl.ds(0, 2)], send_sems.at[7])
+        wait_bytes(products.at[0], send_sems.at[8])
+
+    @pl.when(jnp.logical_not(inner))
+    def _():
+        wait_bytes(products.at[0], send_sems.at[3])
+
     wait_bytes(shares.at[pl.ds(0, SPLIT - 1)], send_sems.at[4])
     wait_bytes(grads.at[pl.ds(0, groups - 1)], send_sems.at[5])
     wait_bytes(total.at[pl.ds(0, SPLIT - 1)], send_sems.at[6])
@@ -292,14 +360,9 @@
     experts = devices // SPLIT
     rows, hidden = gate_pre.shape
     capacity = rows // devices
-    width = cotangent.shape[1]
+    tokens, width = cotangent.shape
     part = width // SPLIT
     piece = part // groups
-
-    ordered = cotangent.reshape(-1, groups, SPLIT, piece).transpose(0, 2, 1, 3).reshape(-1, width)
-    buffer = slot_buffer(ordered, expert_ids, route_weights, experts, capacity)
-    sent = buffer.reshape(experts, capacity // 4, 4, SPLIT, part).transpose(0, 3, 1, 2, 4)
-    sent = sent.reshape(devices, capacity // 4, 4, part)
 
     half = jnp.bfloat16
     vmem = pl.BlockSpec(memory_space=pltpu.VMEM)
@@ -311,9 +374,11 @@
             jax.ShapeDtypeStruct(gate_pre.shape, half),
             jax.ShapeDtypeStruct(gate_pre.shape, half),
         ),
-        in_specs=[vmem] * 4,
+        in_specs=[vmem] * 6,
         out_specs=(vmem, vmem, vmem),
         scratch_shapes=[
+            pltpu.VMEM((SPLIT, tokens, part), half),
+            pltpu.VMEM((experts, SPLIT, capacity // 4, 4, part), half),
             pltpu.VMEM((devices, capacity // 4, 4, part), half),
             pltpu.VMEM((rows, part), half),
             pltpu.VMEM((SPLIT, piece, hidden), half),
@@ -325,7 +390,7 @@
             pltpu.VMEM((groups, SPLIT, piece, hidden), half),
             pltpu.VMEM((SPLIT, piece, hidden), half),
             pltpu.VMEM((SPLIT, piece, hidden), half),
-            dma((7,)),
+            dma((9,)),
             dma((devices,)),
             dma((SPLIT,)),
             dma((groups,)),
@@ -337,7 +402,14 @@
         compiler_params=pltpu.CompilerParams(
             collective_id=0, has_side_effects=True, vmem_limit_bytes=48 * 1024 * 1024
         ),
-    )(sent, gate_pre, up_pre, down_weight)
+    )(
+        cotangent,
+        expert_ids.reshape(1, tokens),
+        route_weights.reshape(1, tokens),
+        gate_pre,
+        up_pre,
+        down_weight,
+    )
 
 
 def solution(mesh):

time: 145 us -> 155 us (1.069)
  Pallas kernels: 134 us -> 147 us
  other arithmetic: 4.79 us -> 0 us
  local copies, waits for them, and re-layouts: 5.3 us -> 6.94 us
    pallas_call x1, Pallas kernels: 134 us -> 147 us  [per_device(): pl.pallas_call(functools.partial(layer_kernel, (groups, devices, ring)),...]
    another operation x1 -> x0, other arithmetic: 3.36 us -> none  [slot_buffer(): earlier = jnp.cumsum(touched, axis=0) - touched]
    unnamed x10 -> x15, local copies, waits for them, and re-layouts: 4.35 us -> 6.94 us
where the time goes in v3:
time: 155 us; the launch traced here: 154 us
  Pallas kernels  147 us (95%)
  local copies, waits for them, and re-layouts  6.94 us (4%)
    pallas_call x1, Pallas kernels, per_device(): pl.pallas_call(functools.partial(layer_kernel, (groups, devices, ring)),...  147 us
    unnamed x15, local copies, waits for them, and re-layouts  6.94 us

profile of v3, /device:TPU:1, one launch (start us, length us, event | category | flops | bytes accessed | tf_op | source)
XLA Modules:
  0.0 154.3 jit_solution(7168919735551597452)
XLA Ops:
  0.6 0.0 copy-start.4
  0.6 0.0 copy-start.5
  0.7 0.6 copy-done.4
  1.3 0.0 copy-done.5
  1.3 0.0 copy-start
  1.3 1.2 copy-done
  2.5 0.0 copy-start.1
  2.5 1.0 copy-done.1
  3.5 0.0 copy-start.2
  3.5 1.0 copy-done.2
  4.5 0.0 copy-start.3
  4.5 0.9 copy-done.3
  5.4 146.7 %shard_map.85 = (bf16[448,256]{1,0:T(8,128)(2,1)S(1)}, bf16[768,256]{1,0:T(8,128)(2,1)S(1)}, bf16[768,256]{1,0:T(8,128)(2,1)S(1)}) custom-call(bf16[128,3584]{1,0:T(8,128)(2,1)S(1)} %copy-done, s32[1,128]{1,0:T(1,128)S(1)} %bitcast.2, f32[1,128]{1,0:T(1,128)S(1)} %bitcast.3, bf16[768,256]{1,0:T(8,128)(2,1)S(1)} %copy-done.1, bf16[768,256]{1,0:T(8,128)(2,1)S(1)} %copy-done.2, ...), custom_call_target="tpu_custom_call" | custom-call | tf_op jit(solution)/shard_map/pallas_call | solution.py:370
  152.2 0.7 copy.12
  152.8 0.7 copy.13
  153.6 0.7 copy.14
Async XLA Ops:
  0.6 0.7 copy-start.4
  0.6 0.7 copy-start.5
  1.3 1.2 copy-start
  2.5 1.0 copy-start.1
  3.5 1.0 copy-start.2
  4.5 0.9 copy-start.3

commit v4 on v3

--- a/solution.py
+++ b/solution.py
@@ -8,7 +8,7 @@
 from jax.sharding import PartitionSpec as P
 
 SPLIT = 4
-PASS_ON = 2
+ORDER = (0, 4, 1, 3, 7, 5, 2, 6)
 MESH = pl.DeviceIdType.MESH
 
 
@@ -65,15 +65,19 @@
 
 def layer_kernel(
     dims,
-    cotangent,
+    cotangent_hbm,
     ids,
     scales,
+    gate_hbm,
+    up_hbm,
+    down_hbm,
+    weight_grad,
+    gate_grad,
+    up_grad,
+    cotangent,
     gate,
     up,
     down,
-    weight_grad,
-    gate_grad,
-    up_grad,
     ordered,
     sent,
     arrived,
@@ -84,6 +88,8 @@
     partial,
     shares,
     grads,
+    pair_parts,
+    pairs,
     grad_parts,
     total,
     grad_rows,
@@ -95,6 +101,9 @@
     share_sems,
     grad_sems,
     total_sems,
+    pair_sems,
+    load_sems,
+    plane_sem,
 ):
     groups, devices, ring = dims
     rows_y = devices // ring
@@ -109,14 +118,28 @@
     q = e % SPLIT
     base = e - q
 
+    loads = [
+        pltpu.make_async_copy(source, target, load_sems.at[at])
+        for at, (source, target) in enumerate(
+            ((gate_hbm, gate), (up_hbm, up), (cotangent_hbm, cotangent), (down_hbm, down))
+        )
+    ]
+    for load in loads:
+        load.start()
+
     def peer(target):
         return {"expert": target}
 
     barrier = pltpu.get_barrier_semaphore()
 
-    @pl.loop(1, devices)
+    @pl.loop(1, ring)
     def _(step):
-        target = lax.rem(e + step, devices)
+        target = y * ring + lax.rem(z + step, ring)
+        pl.semaphore_signal(barrier, inc=1, device_id=peer(target), device_id_type=MESH)
+
+    @pl.loop(1, rows_y)
+    def _(step):
+        target = lax.rem(y + step, rows_y) * ring + z
         pl.semaphore_signal(barrier, inc=1, device_id=peer(target), device_id_type=MESH)
 
     @pl.loop(1, groups)
@@ -124,8 +147,8 @@
         target = lax.rem(i + step, groups)
         pl.semaphore_signal(barrier, inc=1, device_id={"dp": target}, device_id_type=MESH)
 
-    fill_slots(groups, cotangent, ids, scales, ordered, sent)
-    arrived[e] = sent[e // SPLIT, q]
+    loads[0].wait()
+    loads[1].wait()
 
     @pl.loop(0, rows_y)
     def _(step):
@@ -134,8 +157,15 @@
         active = g / (1.0 + jnp.exp(-g))
         products[q, span, :] = (active * up[span, :].astype(jnp.float32)).astype(jnp.bfloat16)
 
+    loads[3].wait()
     own_weight[q] = down[pl.ds(pl.multiple_of(q * piece, 16), piece), :]
-    pl.semaphore_wait(barrier, devices - 1 + groups - 1)
+    pl.semaphore_wait(barrier, ring - 1 + rows_y - 1 + groups - 1)
+
+    @pl.loop(1, ring)
+    def _(step):
+        target = y * ring + lax.rem(z + step, ring)
+        pl.semaphore_signal(plane_sem, inc=1, device_id=peer(target), device_id_type=MESH)
+
 
     for step in range(1, SPLIT):
         other = lax.rem(q + step, SPLIT)
@@ -168,46 +198,87 @@
     def _():
         product_to(q, q - 1, 3)
 
+    loads[2].wait()
+    fill_slots(groups, cotangent, ids, scales, ordered, sent)
+    arrived[e] = sent[e // SPLIT, q]
+    pl.semaphore_wait(plane_sem, ring - 1)
+
     def away(step, count):
-        return jnp.where(step % 2 == 1, (step + 1) // 2, count - step // 2)
-
-    @pl.loop(0, devices)
-    def _(step):
-        to_y = lax.rem(y + away(step // ring, rows_y), rows_y)
-        to_z = lax.rem(z + away(step % ring, ring), ring)
-        target = to_y * ring + to_z
-
-        @pl.when(target != e)
-        def _():
-            pltpu.make_async_remote_copy(
-                src_ref=sent.at[target // SPLIT, target % SPLIT],
-                dst_ref=arrived.at[e],
-                send_sem=send_sems.at[1],
-                recv_sem=token_sems.at[e],
-                device_id=peer(target),
-                device_id_type=MESH,
-            ).start()
+        if count != 8:
+            return step
+        return sum(jnp.where(step == k, far, 0) for k, far in enumerate(ORDER))
+
+    def send_tokens(first, last):
+        @pl.loop(first * ring, last * ring)
+        def _(step):
+            to_y = lax.rem(y + away(step // ring, rows_y), rows_y)
+            to_z = lax.rem(z + away(step % ring, ring), ring)
+            target = to_y * ring + to_z
+
+            @pl.when(target != e)
+            def _():
+                pltpu.make_async_remote_copy(
+                    src_ref=sent.at[target // SPLIT, target % SPLIT],
+                    dst_ref=arrived.at[e],
+                    send_sem=send_sems.at[1],
+                    recv_sem=token_sems.at[e],
+                    device_id=peer(target),
+                    device_id_type=MESH,
+                ).start()
+
+    send_tokens(0, rows_y // 2)
 
     for step in range(1, SPLIT):
         other = lax.rem(q + step, SPLIT)
         wait_bytes(own_weight.at[other], quad_weight_sems.at[other])
     weight[i] = own_weight[...]
 
-    @pl.loop(1, groups)
-    def _(step):
-        target = lax.rem(i + step, groups)
+    chips = groups // 2
+    chip, core = i // 2, i % 2
+    sibling = {"dp": chip * 2 + 1 - core}
+
+    for hop in range(1, chips):
         pltpu.make_async_remote_copy(
-            src_ref=own_weight,
+            src_ref=weight.at[i],
             dst_ref=weight.at[i],
             send_sem=send_sems.at[2],
             recv_sem=weight_sems.at[i],
-            device_id={"dp": target},
+            device_id={"dp": lax.rem(chip + hop, chips) * 2 + core},
             device_id_type=MESH,
         ).start()
 
-    @pl.loop(1, groups)
-    def _(step):
-        source = lax.rem(i + step, groups)
+    def weight_over(block):
+        pltpu.make_async_remote_copy(
+            src_ref=weight.at[block],
+            dst_ref=weight.at[block],
+            send_sem=send_sems.at[9],
+            recv_sem=weight_sems.at[block],
+            device_id=sibling,
+            device_id_type=MESH,
+        ).start()
+
+    weight_over(i)
+
+    @pl.when(inner)
+    def _():
+        for way in (1, -1):
+            wait_bytes(products.at[q - way], product_sems.at[q - way])
+            product_to(q - way, q + way, 7)
+
+    send_tokens(rows_y // 2, rows_y)
+    far = jnp.where(q == 1, SPLIT - 1, 0)
+
+    @pl.when(inner)
+    def _():
+        wait_bytes(products.at[far], product_sems.at[far])
+        product_to(far, jnp.where(q == 1, 0, SPLIT - 1), 8)
+
+    for hop in range(1, chips):
+        source = lax.rem(chip + chips - hop, chips) * 2 + core
+        wait_bytes(weight.at[source], weight_sems.at[source])
+        weight_over(source)
+    for hop in range(chips):
+        source = lax.rem(chip + chips - hop, chips) * 2 + 1 - core
         wait_bytes(weight.at[source], weight_sems.at[source])
 
     @pl.loop(0, rows_y)
@@ -221,12 +292,6 @@
             @pl.when(source != e)
             def _():
                 wait_bytes(arrived.at[source], token_sems.at[source])
-
-        @pl.when(inner & (step == min(PASS_ON, rows_y - 1)))
-        def _():
-            for way in (1, -1):
-                wait_bytes(products.at[q - way], product_sems.at[q - way])
-                product_to(q - way, q + way, 7)
 
         block = arrived[pl.ds(from_y * ring, ring)].reshape(chunk, part)
         span = pl.ds(pl.multiple_of(from_y * chunk, 16), chunk)
@@ -247,87 +312,108 @@
                 device_id_type=MESH,
             ).start()
 
-    far = jnp.where(q == 1, SPLIT - 1, 0)
-
-    @pl.when(inner)
-    def _():
-        wait_bytes(products.at[far], product_sems.at[far])
-        product_to(far, jnp.where(q == 1, 0, SPLIT - 1), 8)
-
-    @pl.when(jnp.logical_not(inner))
-    def _():
-        for step in range(1, SPLIT):
-            other = lax.rem(q + step, SPLIT)
-            wait_bytes(products.at[other], product_sems.at[other])
-
-    @pl.loop(0, SPLIT)
-    def _(j):
-        grads[:, j] = (
-            lax.dot_general(
-                routed[...],
-                products[j],
-                (((0,), (0,)), ((), ())),
-                preferred_element_type=jnp.float32,
-            )
-            .astype(jnp.bfloat16)
-            .reshape(groups, piece, hidden)
-        )
-
-    grad_parts[i] = grads[i]
-
-    @pl.loop(1, groups)
-    def _(step):
-        target = lax.rem(i + step, groups)
+    def slice_of(turn):
+        j = jnp.where(turn == 3, q, jnp.where(q < 2, SPLIT - 1, 0))
+        j = jnp.where(turn == 2, jnp.where(q < 2, 2, 1), j)
+        return jnp.where(turn == 1, q + 1 - 2 * (q % 2), j)
+
+    def pair_up(turn):
+        j = slice_of(turn)
+        wait_bytes(pair_parts.at[j], pair_sems.at[j])
+        for at in range(chips):
+            pair = grads[j, core, at].astype(jnp.float32)
+            pair = pair + pair_parts[j, at].astype(jnp.float32)
+            pairs[j, at] = pair.astype(jnp.bfloat16)
+        grad_parts[j, chip] = pairs[j, chip]
+        for hop in range(1, chips):
+            target = lax.rem(chip + hop, chips)
+            pltpu.make_async_remote_copy(
+                src_ref=pairs.at[j, target],
+                dst_ref=grad_parts.at[j, chip],
+                send_sem=send_sems.at[5],
+                recv_sem=grad_sems.at[j, chip],
+                device_id={"dp": target * 2 + core},
+                device_id_type=MESH,
+            ).start()
+
+    @pl.loop(1, SPLIT + 1)
+    def _(turn):
+        j = slice_of(turn)
+
+        @pl.when((j != q) & jnp.logical_not(inner))
+        def _():
+            wait_bytes(products.at[j], product_sems.at[j])
+
+        slice_grads = lax.dot_general(
+            routed[...],
+            products[j],
+            (((0,), (0,)), ((), ())),
+            preferred_element_type=jnp.float32,
+        ).astype(jnp.bfloat16)
+        for at in range(groups):
+            grads[j, at % 2, at // 2] = slice_grads[at * piece : (at + 1) * piece]
         pltpu.make_async_remote_copy(
-            src_ref=grads.at[target],
-            dst_ref=grad_parts.at[i],
-            send_sem=send_sems.at[5],
-            recv_sem=grad_sems.at[i],
-            device_id={"dp": target},
+            src_ref=grads.at[j, 1 - core],
+            dst_ref=pair_parts.at[j],
+            send_sem=send_sems.at[10],
+            recv_sem=pair_sems.at[j],
+            device_id=sibling,
             device_id_type=MESH,
         ).start()
 
-    @pl.loop(0, rows_y)
-    def _(step):
-        from_y = lax.rem(y + rows_y - lax.rem(away(step, rows_y), rows_y), rows_y)
-        span = pl.ds(pl.multiple_of(from_y * chunk, 16), chunk)
-        for hop in range(1, SPLIT):
-            other = lax.rem(q + hop, SPLIT)
-            wait_bytes(shares.at[other, span], share_sems.at[other, from_y])
-        upstream = shares[0, span, :].astype(jnp.float32)
-        for j in range(1, SPLIT):
-            upstream = upstream + shares[j, span, :].astype(jnp.float32)
-        g = gate[span, :].astype(jnp.float32)
-        u = up[span, :].astype(jnp.float32)
-        sigmoid = 1.0 / (1.0 + jnp.exp(-g))
-        gate_grad[span, :] = (upstream * u * sigmoid * (1.0 + g * (1.0 - sigmoid))).astype(
-            jnp.bfloat16
-        )
-        up_grad[span, :] = (upstream * (g * sigmoid)).astype(jnp.bfloat16)
-
-    @pl.loop(1, groups)
-    def _(step):
-        source = lax.rem(i + step, groups)
-        wait_bytes(grad_parts.at[source], grad_sems.at[source])
-
-    @pl.loop(0, SPLIT)
-    def _(j):
-        whole = grad_parts[0, j].astype(jnp.float32)
-        for k in range(1, groups):
-            whole = whole + grad_parts[k, j].astype(jnp.float32)
+        @pl.when(turn > 1)
+        def _():
+            pair_up(turn - 1)
+
+    pair_up(SPLIT)
+
+    def finish(first, last):
+        @pl.loop(first, last)
+        def _(step):
+            from_y = lax.rem(y + rows_y - lax.rem(away(step, rows_y), rows_y), rows_y)
+            span = pl.ds(pl.multiple_of(from_y * chunk, 16), chunk)
+            for hop in range(1, SPLIT):
+                other = lax.rem(q + hop, SPLIT)
+                wait_bytes(shares.at[other, span], share_sems.at[other, from_y])
+            upstream = shares[0, span, :].astype(jnp.float32)
+            for j in range(1, SPLIT):
+                upstream = upstream + shares[j, span, :].astype(jnp.float32)
+            g = gate[span, :].astype(jnp.float32)
+            u = up[span, :].astype(jnp.float32)
+            sigmoid = 1.0 / (1.0 + jnp.exp(-g))
+            gate_grad[span, :] = (upstream * u * sigmoid * (1.0 + g * (1.0 - sigmoid))).astype(
+                jnp.bfloat16
+            )
+            up_grad[span, :] = (upstream * (g * sigmoid)).astype(jnp.bfloat16)
+
+    early = rows_y - rows_y // 4
+    finish(0, early)
+
+    @pl.loop(1, SPLIT + 1)
+    def _(turn):
+        j = slice_of(turn)
+        for hop in range(1, chips):
+            source = lax.rem(chip + hop, chips)
+            wait_bytes(grad_parts.at[j, source], grad_sems.at[j, source])
+
+        whole = grad_parts[j, 0].astype(jnp.float32)
+        for k in range(1, chips):
+            whole = whole + grad_parts[j, k].astype(jnp.float32)
         total[j] = whole.astype(jnp.bfloat16)
 
+        @pl.when(j != q)
+        def _():
+            pltpu.make_async_remote_copy(
+                src_ref=total.at[j],
+                dst_ref=grad_rows.at[q],
+                send_sem=send_sems.at[6],
+                recv_sem=total_sems.at[q],
+                device_id=peer(base + j),
+                device_id_type=MESH,
+            ).start()
+
     grad_rows[q] = total[q]
-    for step in range(1, SPLIT):
-        other = lax.rem(q + step, SPLIT)
-        pltpu.make_async_remote_copy(
-            src_ref=total.at[other],
-            dst_ref=grad_rows.at[q],
-            send_sem=send_sems.at[6],
-            recv_sem=total_sems.at[q],
-            device_id=peer(base + other),
-            device_id_type=MESH,
-        ).start()
+    finish(early, rows_y)
     for step in range(1, SPLIT):
         other = lax.rem(q + step, SPLIT)
         wait_bytes(grad_rows.at[other], total_sems.at[other])
@@ -336,7 +422,11 @@
 
     wait_bytes(own_weight.at[pl.ds(0, SPLIT - 1)], send_sems.at[0])
     wait_bytes(arrived.at[pl.ds(0, devices - 1)], send_sems.at[1])
-    wait_bytes(weight.at[pl.ds(0, groups - 1)], send_sems.at[2])
+    if chips > 1:
+        wait_bytes(weight.at[pl.ds(0, chips - 1)], send_sems.at[2])
+        wait_bytes(pairs.at[:, pl.ds(0, chips - 1)], send_sems.at[5])
+    wait_bytes(weight.at[pl.ds(0, chips)], send_sems.at[9])
+    wait_bytes(pair_parts, send_sems.at[10])
 
     @pl.when(inner)
     def _():
@@ -349,7 +439,6 @@
         wait_bytes(products.at[0], send_sems.at[3])
 
     wait_bytes(shares.at[pl.ds(0, SPLIT - 1)], send_sems.at[4])
-    wait_bytes(grads.at[pl.ds(0, groups - 1)], send_sems.at[5])
     wait_bytes(total.at[pl.ds(0, SPLIT - 1)], send_sems.at[6])
 
 
@@ -366,6 +455,7 @@
 
     half = jnp.bfloat16
     vmem = pl.BlockSpec(memory_space=pltpu.VMEM)
+    hbm = pl.BlockSpec(memory_space=pl.ANY)
     dma = pltpu.SemaphoreType.DMA
     return pl.pallas_call(
         functools.partial(layer_kernel, (groups, devices, ring)),
@@ -374,9 +464,13 @@
             jax.ShapeDtypeStruct(gate_pre.shape, half),
             jax.ShapeDtypeStruct(gate_pre.shape, half),
         ),
-        in_specs=[vmem] * 6,
+        in_specs=[hbm, vmem, vmem, hbm, hbm, hbm],
         out_specs=(vmem, vmem, vmem),
         scratch_shapes=[
+            pltpu.VMEM((tokens, width), half),
+            pltpu.VMEM((rows, hidden), half),
+            pltpu.VMEM((rows, hidden), half),
+            pltpu.VMEM(down_weight.shape, half),
             pltpu.VMEM((SPLIT, tokens, part), half),
             pltpu.VMEM((experts, SPLIT, capacity // 4, 4, part), half),
             pltpu.VMEM((devices, capacity // 4, 4, part), half),
@@ -386,21 +480,26 @@
             pltpu.VMEM((SPLIT, rows, hidden), half),
             pltpu.VMEM((SPLIT, rows, hidden), half),
             pltpu.VMEM((SPLIT, rows, hidden), half),
-            pltpu.VMEM((groups, SPLIT, piece, hidden), half),
-            pltpu.VMEM((groups, SPLIT, piece, hidden), half),
+            pltpu.VMEM((SPLIT, 2, groups // 2, piece, hidden), half),
+            pltpu.VMEM((SPLIT, groups // 2, piece, hidden), half),
+            pltpu.VMEM((SPLIT, groups // 2, piece, hidden), half),
+            pltpu.VMEM((SPLIT, groups // 2, piece, hidden), half),
             pltpu.VMEM((SPLIT, piece, hidden), half),
             pltpu.VMEM((SPLIT, piece, hidden), half),
-            dma((9,)),
+            dma((11,)),
             dma((devices,)),
             dma((SPLIT,)),
             dma((groups,)),
             dma((SPLIT,)),
             dma((SPLIT, devices // ring)),
-            dma((groups,)),
+            dma((SPLIT, groups // 2)),
             dma((SPLIT,)),
+            dma((SPLIT,)),
+            dma((4,)),
+            pltpu.SemaphoreType.REGULAR,
         ],
         compiler_params=pltpu.CompilerParams(
-            collective_id=0, has_side_effects=True, vmem_limit_bytes=48 * 1024 * 1024
+            collective_id=0, has_side_effects=True, vmem_limit_bytes=62 * 1024 * 1024
         ),
     )(
         cotangent,

time: 155 us -> 120 us (0.77)
  the two profiles are of different devices: /device:TPU:1 before, /device:TPU:44 now
where the time goes in v4:
time: 120 us
  Pallas kernels  116 us (97%)
  local copies, waits for them, and re-layouts  3.58 us (3%)
    pallas_call x1, Pallas kernels, per_device(): pl.pallas_call(functools.partial(layer_kernel, (groups, devices, ring)),...  116 us
    unnamed x7, local copies, waits for them, and re-layouts  3.58 us

profile of v4, /device:TPU:44, one launch (start us, length us, event | category | flops | bytes accessed | tf_op | source)
XLA Modules:
  0.0 120.0 jit_solution(13806820817708662910)
XLA Ops:
  0.6 115.8 %shard_map.85 = (bf16[448,256]{1,0:T(8,128)(2,1)}, bf16[768,256]{1,0:T(8,128)(2,1)}, bf16[768,256]{1,0:T(8,128)(2,1)}) custom-call(bf16[128,3584]{1,0:T(8,128)(2,1)} %cotangent_hbm.1, s32[1,128]{1,0:T(1,128)} %bitcast.2, f32[1,128]{1,0:T(1,128)} %bitcast.3, bf16[768,256]{1,0:T(8,128)(2,1)} %gate_hbm.1, bf16[768,256]{1,0:T(8,128)(2,1)} %up_hbm.1, ...), custom_call_target="tpu_custom_call" | custom-call | tf_op jit(solution)/shard_map/pallas_call | solution.py:460
  116.4 0.0 copy-start.1
  116.4 1.7 %copy.12 = bf16[448,256]{1,0:T(8,128)(2,1)} copy(bf16[448,256]{1,0:T(8,128)(2,1)} %get-tuple-element.6) | data formatting | bytes 458752
  118.1 0.0 copy-done.1
  118.1 0.0 copy-start
  118.1 0.7 copy.13
  118.9 0.4 copy-done
  119.3 0.7 copy.14
Async XLA Ops:
  116.4 1.7 %copy-start.1 = (bf16[768,256]{1,0:T(8,128)(2,1)S(1)}, bf16[768,256]{1,0:T(8,128)(2,1)}, u32[]{:S(2)}) copy-start(bf16[768,256]{1,0:T(8,128)(2,1)} %get-tuple-element.7) | copy-start | bytes 1179652
  118.1 1.1 copy-start

commit v5 on v4

--- a/solution.py
+++ b/solution.py
@@ -87,6 +87,7 @@
     products,
     partial,
     shares,
+    pass_in,
     grads,
     pair_parts,
     pairs,
@@ -104,6 +105,7 @@
     pair_sems,
     load_sems,
     plane_sem,
+    pass_sems,
 ):
     groups, devices, ring = dims
     rows_y = devices // ring
@@ -259,13 +261,14 @@
 
     weight_over(i)
 
+    send_tokens(rows_y // 2, 3 * rows_y // 4)
     @pl.when(inner)
     def _():
         for way in (1, -1):
             wait_bytes(products.at[q - way], product_sems.at[q - way])
             product_to(q - way, q + way, 7)
 
-    send_tokens(rows_y // 2, rows_y)
+    send_tokens(3 * rows_y // 4, rows_y)
     far = jnp.where(q == 1, SPLIT - 1, 0)
 
     @pl.when(inner)
@@ -281,6 +284,32 @@
         source = lax.rem(chip + chips - hop, chips) * 2 + 1 - core
         wait_bytes(weight.at[source], weight_sems.at[source])
 
+    mate = q + 1 - 2 * (q % 2)
+    fars = (jnp.where(q < 2, 2, 1), jnp.where(q < 2, SPLIT - 1, 0))
+
+    def rows_of(step):
+        from_y = lax.rem(y + rows_y - lax.rem(away(step, rows_y), rows_y), rows_y)
+        return from_y, pl.ds(pl.multiple_of(from_y * chunk, 16), chunk)
+
+    def share_to(source, target, stage, arrival, other):
+        pltpu.make_async_remote_copy(
+            src_ref=source,
+            dst_ref=target,
+            send_sem=send_sems.at[stage],
+            recv_sem=arrival,
+            device_id=peer(base + other),
+            device_id_type=MESH,
+        ).start()
+
+    def pass_on(step):
+        from_y, span = rows_of(step)
+        for n in range(2):
+            wait_bytes(pass_in.at[n, span], pass_sems.at[n, from_y])
+            both = partial[fars[n], span, :].astype(jnp.float32)
+            both = both + pass_in[n, span, :].astype(jnp.float32)
+            partial[fars[n], span, :] = both.astype(jnp.bfloat16)
+            share_to(partial.at[fars[n], span], shares.at[1, span], 12, share_sems.at[1, from_y], fars[n])
+
     @pl.loop(0, rows_y)
     def _(step):
         from_y = lax.rem(y + rows_y - lax.rem(away(step, rows_y), rows_y), rows_y)
@@ -300,17 +329,13 @@
             partial[j, span, :] = jnp.dot(
                 block, weight[:, j].reshape(part, hidden), preferred_element_type=jnp.float32
             ).astype(jnp.bfloat16)
-        shares[q, span, :] = partial[q, span, :]
-        for hop in range(1, SPLIT):
-            other = lax.rem(q + hop, SPLIT)
-            pltpu.make_async_remote_copy(
-                src_ref=partial.at[other, span],
-                dst_ref=shares.at[q, span],
-                send_sem=send_sems.at[4],
-                recv_sem=share_sems.at[q, from_y],
-                device_id=peer(base + other),
-                device_id_type=MESH,
-            ).start()
+
+        @pl.when(jnp.logical_not(inner))
+        def _():
+            for n in range(2):
+                share_to(partial.at[fars[n], span], pass_in.at[n, span], 11, pass_sems.at[n, from_y], mate)
+
+        share_to(partial.at[mate, span], shares.at[0, span], 4, share_sems.at[0, from_y], mate)
 
     def slice_of(turn):
         j = jnp.where(turn == 3, q, jnp.where(q < 2, SPLIT - 1, 0))
@@ -365,6 +390,12 @@
         def _():
             pair_up(turn - 1)
 
+        @pl.when(inner)
+        def _():
+            @pl.loop((turn - 1) * rows_y // 4, turn * rows_y // 4)
+            def _(step):
+                pass_on(step)
+
     pair_up(SPLIT)
 
     def finish(first, last):
@@ -372,12 +403,10 @@
         def _(step):
             from_y = lax.rem(y + rows_y - lax.rem(away(step, rows_y), rows_y), rows_y)
             span = pl.ds(pl.multiple_of(from_y * chunk, 16), chunk)
-            for hop in range(1, SPLIT):
-                other = lax.rem(q + hop, SPLIT)
-                wait_bytes(shares.at[other, span], share_sems.at[other, from_y])
-            upstream = shares[0, span, :].astype(jnp.float32)
-            for j in range(1, SPLIT):
-                upstream = upstream + shares[j, span, :].astype(jnp.float32)
+            upstream = partial[q, span, :].astype(jnp.float32)
+            for n in range(2):
+                wait_bytes(shares.at[n, span], share_sems.at[n, from_y])
+                upstream = upstream + shares[n, span, :].astype(jnp.float32)
             g = gate[span, :].astype(jnp.float32)
             u = up[span, :].astype(jnp.float32)
             sigmoid = 1.0 / (1.0 + jnp.exp(-g))
@@ -438,7 +467,16 @@
     def _():
         wait_bytes(products.at[0], send_sems.at[3])
 
-    wait_bytes(shares.at[pl.ds(0, SPLIT - 1)], send_sems.at[4])
+    wait_bytes(shares.at[0], send_sems.at[4])
+
+    @pl.when(inner)
+    def _():
+        wait_bytes(shares, send_sems.at[12])
+
+    @pl.when(jnp.logical_not(inner))
+    def _():
+        wait_bytes(shares, send_sems.at[11])
+
     wait_bytes(total.at[pl.ds(0, SPLIT - 1)], send_sems.at[6])
 
 
@@ -479,24 +517,26 @@
             pltpu.VMEM((groups, SPLIT, piece, hidden), half),
             pltpu.VMEM((SPLIT, rows, hidden), half),
             pltpu.VMEM((SPLIT, rows, hidden), half),
-            pltpu.VMEM((SPLIT, rows, hidden), half),
+            pltpu.VMEM((2, rows, hidden), half),
+            pltpu.VMEM((2, rows, hidden), half),
             pltpu.VMEM((SPLIT, 2, groups // 2, piece, hidden), half),
             pltpu.VMEM((SPLIT, groups // 2, piece, hidden), half),
             pltpu.VMEM((SPLIT, groups // 2, piece, hidden), half),
             pltpu.VMEM((SPLIT, groups // 2, piece, hidden), half),
             pltpu.VMEM((SPLIT, piece, hidden), half),
             pltpu.VMEM((SPLIT, piece, hidden), half),
-            dma((11,)),
+            dma((13,)),
             dma((devices,)),
             dma((SPLIT,)),
             dma((groups,)),
             dma((SPLIT,)),
-            dma((SPLIT, devices // ring)),
+            dma((2, devices // ring)),
             dma((SPLIT, groups // 2)),
             dma((SPLIT,)),
             dma((SPLIT,)),
             dma((4,)),
             pltpu.SemaphoreType.REGULAR,
+            dma((2, devices // ring)),
         ],
         compiler_params=pltpu.CompilerParams(
             collective_id=0, has_side_effects=True, vmem_limit_bytes=62 * 1024 * 1024

time: 120 us -> 104 us (0.87)
  the two profiles are of different devices: /device:TPU:44 before, /device:TPU:1 now
where the time goes in v5:
time: 104 us
  Pallas kernels  99.8 us (96%)
  local copies, waits for them, and re-layouts  3.58 us (3%)
    pallas_call x1, Pallas kernels, per_device(): pl.pallas_call(functools.partial(layer_kernel, (groups, devices, ring)),...  99.8 us
    unnamed x7, local copies, waits for them, and re-layouts  3.58 us

profile of v5, /device:TPU:1, one launch (start us, length us, event | category | flops | bytes accessed | tf_op | source)
XLA Modules:
  0.0 104.0 jit_solution(17029984312040230658)
XLA Ops:
  0.6 99.8 %shard_map.85 = (bf16[448,256]{1,0:T(8,128)(2,1)}, bf16[768,256]{1,0:T(8,128)(2,1)}, bf16[768,256]{1,0:T(8,128)(2,1)}) custom-call(bf16[128,3584]{1,0:T(8,128)(2,1)} %cotangent_hbm.1, s32[1,128]{1,0:T(1,128)} %bitcast.2, f32[1,128]{1,0:T(1,128)} %bitcast.3, bf16[768,256]{1,0:T(8,128)(2,1)} %gate_hbm.1, bf16[768,256]{1,0:T(8,128)(2,1)} %up_hbm.1, ...), custom_call_target="tpu_custom_call" | custom-call | tf_op jit(solution)/shard_map/pallas_call | solution.py:498
  100.4 0.0 copy-start.1
  100.4 1.7 %copy.12 = bf16[448,256]{1,0:T(8,128)(2,1)} copy(bf16[448,256]{1,0:T(8,128)(2,1)} %get-tuple-element.6) | data formatting | bytes 458752
  102.1 0.0 copy-done.1
  102.1 0.0 copy-start
  102.1 0.7 copy.13
  102.8 0.4 copy-done
  103.2 0.7 copy.14
Async XLA Ops:
  100.4 1.7 %copy-start.1 = (bf16[768,256]{1,0:T(8,128)(2,1)S(1)}, bf16[768,256]{1,0:T(8,128)(2,1)}, u32[]{:S(2)}) copy-start(bf16[768,256]{1,0:T(8,128)(2,1)} %get-tuple-element.7) | copy-start | bytes 1179652
  102.1 1.1 %copy-start = (bf16[768,256]{1,0:T(8,128)(2,1)S(1)}, bf16[768,256]{1,0:T(8,128)(2,1)}, u32[]{:S(2)}) copy-start(bf16[768,256]{1,0:T(8,128)(2,1)} %get-tuple-element.8) | copy-start | bytes 1179652

commit v6 on v5

--- a/solution.py
+++ b/solution.py
@@ -262,13 +262,13 @@
     weight_over(i)
 
     send_tokens(rows_y // 2, 3 * rows_y // 4)
+    send_tokens(3 * rows_y // 4, rows_y)
     @pl.when(inner)
     def _():
         for way in (1, -1):
             wait_bytes(products.at[q - way], product_sems.at[q - way])
             product_to(q - way, q + way, 7)
 
-    send_tokens(3 * rows_y // 4, rows_y)
     far = jnp.where(q == 1, SPLIT - 1, 0)
 
     @pl.when(inner)
@@ -415,7 +415,7 @@
             )
             up_grad[span, :] = (upstream * (g * sigmoid)).astype(jnp.bfloat16)
 
-    early = rows_y - rows_y // 4
+    early = rows_y // 4
     finish(0, early)
 
     @pl.loop(1, SPLIT + 1)

time: 104 us -> 103 us (level); the launches traced: 104 us -> 101 us
  Pallas kernels: 99.8 us -> 97.2 us
    pallas_call x1, Pallas kernels: 99.8 us -> 97.2 us  [per_device(): pl.pallas_call(functools.partial(layer_kernel, (groups, devices, ring)),...]
where the time goes in v6:
time: 103 us; the launch traced here: 101 us
  Pallas kernels  97.2 us (94%)
  local copies, waits for them, and re-layouts  3.58 us (3%)
    pallas_call x1, Pallas kernels, per_device(): pl.pallas_call(functools.partial(layer_kernel, (groups, devices, ring)),...  97.2 us
    unnamed x7, local copies, waits for them, and re-layouts  3.58 us

profile of v6, /device:TPU:1, one launch (start us, length us, event | category | flops | bytes accessed | tf_op | source)
XLA Modules:
  0.0 101.4 jit_solution(11997193767481001159)
XLA Ops:
  0.6 97.2 %shard_map.85 = (bf16[448,256]{1,0:T(8,128)(2,1)}, bf16[768,256]{1,0:T(8,128)(2,1)}, bf16[768,256]{1,0:T(8,128)(2,1)}) custom-call(bf16[128,3584]{1,0:T(8,128)(2,1)} %cotangent_hbm.1, s32[1,128]{1,0:T(1,128)} %bitcast.2, f32[1,128]{1,0:T(1,128)} %bitcast.3, bf16[768,256]{1,0:T(8,128)(2,1)} %gate_hbm.1, bf16[768,256]{1,0:T(8,128)(2,1)} %up_hbm.1, ...), custom_call_target="tpu_custom_call" | custom-call | tf_op jit(solution)/shard_map/pallas_call | solution.py:498
  97.8 0.0 copy-start.1
  97.8 1.7 %copy.12 = bf16[448,256]{1,0:T(8,128)(2,1)} copy(bf16[448,256]{1,0:T(8,128)(2,1)} %get-tuple-element.6) | data formatting | bytes 458752
  99.5 0.0 copy-done.1
  99.5 0.0 copy-start
  99.5 0.7 copy.13
  100.3 0.4 copy-done
  100.6 0.7 copy.14
Async XLA Ops:
  97.8 1.7 %copy-start.1 = (bf16[768,256]{1,0:T(8,128)(2,1)S(1)}, bf16[768,256]{1,0:T(8,128)(2,1)}, u32[]{:S(2)}) copy-start(bf16[768,256]{1,0:T(8,128)(2,1)} %get-tuple-element.7) | copy-start | bytes 1179652
  99.5 1.1 %copy-start = (bf16[768,256]{1,0:T(8,128)(2,1)S(1)}, bf16[768,256]{1,0:T(8,128)(2,1)}, u32[]{:S(2)}) copy-start(bf16[768,256]{1,0:T(8,128)(2,1)} %get-tuple-element.8) | copy-start | bytes 1179652
